TPU v7x, 32 devices: a whole 2x2x4 slice. The times are simulated.
32 devices in a mesh: vocab: 16 (over z, y, x), dp: 2 (over core).
Axes of the slice: x: 2, y: 2, z: 4, core: 2. Of those that a mesh axis runs over, the one named last changes fastest.
Arguments:
- embed_table: bfloat16 [16384, 4096], P('vocab'), may hold values from -3 to 3
- token_ids: int32 [2, 16384], P('dp', 'vocab'), may hold values from 0 to 16383, as said below
- grad_rows: bfloat16 [2, 16384, 4096], P('dp', 'vocab'), may hold values from -12 to 12
Outputs:
- updated: bfloat16 [16384, 4096], P('vocab', 'dp')
- grad_rms: float32 [1], replicated
Inputs may be any that keep to these rules, and one draw needn't show every extreme that they name: `token_ids`: rows are read cyclically: row r stands for every r + k * 16384. The window of vocab index v (tokens v * 1024 to (v + 1) * 1024 - 1 of a replica) holds ids that, read as the cyclic representatives from v * 1024 - 256 to (v + 1) * 1024 + 255, rise (never fall) along its tokens; both ends are reached in some window. Only its first 128 and last 128 tokens may lie outside rows v * 1024 to (v + 1) * 1024 - 1 (so read), the first ones below, the last ones above; in every window its first token lies below and its last above, in some window all first 128 lie below, in some all last 128 above.
All inputs are finite; a program needn't handle non-finite values.
Results may differ from a plain program's by a relative error of at most 0.002.
Values may be sent and summed in bfloat16 or wider, within the bound.
A program may use at most 128 MiB of HBM per device.

v0:
```python
import functools

import jax
import jax.numpy as jnp
from jax import lax
from jax.experimental import pallas as pl
from jax.experimental.pallas import tpu as pltpu
from jax.sharding import PartitionSpec as P

MESH = pl.DeviceIdType.MESH
TOK_EDGE = 128
EDGE = 256
COLS = 512
STORE_ROWS = 64

step_rate = 0.5
norm_limit = 1.0


def kernel(sizes, table_ref, ids_ref, grad_ref, grad, table, norm_ref,
           toks, halo, own_ids, mate_ids, halo_ids, square, sums,
           own_sem, own_id_sem, table_sem, mate_sem, mate_id_sem, halo_send, halo_recv,
           halo_id_send, halo_id_recv, sum_send, sum_recv, known_sem):
    n_vocab, n_dp = sizes
    rows, width = table_ref.shape
    tokens = ids_ref.shape[1]
    half = width // n_dp
    n = n_vocab * n_dp
    chunks = half // COLS
    blocks = rows // EDGE
    v = lax.axis_index("vocab")
    p = lax.axis_index("dp")
    me = v * n_dp + p
    mate = 1 - p
    below = lax.rem(v + n_vocab - 1, n_vocab)
    above = lax.rem(v + 1, n_vocab)

    def columns(core, chunk):
        return pl.ds(pl.multiple_of(core * half + chunk * COLS, COLS), COLS)

    def around(distance):
        ahead = v + distance
        return jnp.where(ahead >= n_vocab, ahead - n_vocab, ahead)

    own_half = pl.ds(pl.multiple_of(p * half, half), half)
    own_copy = pltpu.make_async_copy(
        grad_ref.at[0, :, own_half], toks.at[pl.ds(0, tokens), :], own_sem
    )
    own_copy.start()
    own_id_copy = pltpu.make_async_copy(ids_ref, own_ids, own_id_sem)
    own_id_copy.start()
    table_copy = pltpu.make_async_copy(table_ref.at[:, own_half], table, table_sem)

    barrier = pltpu.get_barrier_semaphore()

    greeted = [(v, mate)] + [(w, core) for w in (below, above) for core in range(n_dp)]
    for w, core in greeted:
        pl.semaphore_signal(
            barrier, inc=1, device_id={"vocab": w, "dp": core}, device_id_type=MESH
        )
    pl.semaphore_wait(barrier, len(greeted))

    def remote(src, dst, send, recv, device):
        return pltpu.make_async_remote_copy(
            src_ref=src, dst_ref=dst, send_sem=send, recv_sem=recv,
            device_id=device, device_id_type=MESH,
        )

    sent = []
    mate_id_copy = remote(
        ids_ref, mate_ids, mate_id_sem.at[0], mate_id_sem.at[1], {"vocab": v, "dp": mate}
    )
    mate_id_copy.start()
    sides = ((0, 0, below), (1, tokens - TOK_EDGE, above))
    for side, first, target in sides:
        for core in range(n_dp):
            copy = remote(
                ids_ref.at[:, pl.ds(first, TOK_EDGE)], halo_ids.at[side, p],
                halo_id_send.at[side, core], halo_id_recv.at[side, p],
                {"vocab": target, "dp": core},
            )
            copy.start()
            sent.append(copy)
    mate_copies = []
    for chunk in range(chunks):
        for side, first, target in sides:
            for core in range(n_dp):
                copy = remote(
                    grad_ref.at[0, pl.ds(first, TOK_EDGE), columns(core, chunk)],
                    halo.at[side, p, :, pl.ds(chunk * COLS, COLS)],
                    halo_send.at[side, core, chunk], halo_recv.at[side, p, chunk],
                    {"vocab": target, "dp": core},
                )
                copy.start()
                sent.append(copy)
        copy = remote(
            grad_ref.at[0, :, columns(mate, chunk)],
            toks.at[pl.ds(tokens, tokens), pl.ds(chunk * COLS, COLS)],
            mate_sem.at[0, chunk], mate_sem.at[1, chunk], {"vocab": v, "dp": mate},
        )
        copy.start()
        mate_copies.append(copy)
    table_copy.start()

    own_start = v * rows

    def local(ids):
        shifted = ids - own_start
        return jnp.where(shifted < 0, shifted + n_vocab * rows, shifted)

    def onehot(ids, base, count):
        index = lax.broadcasted_iota(jnp.int32, (count, ids.shape[1]), 0) + base
        return jnp.where(ids == index, 1.0, 0.0).astype(jnp.bfloat16)

    def add_squares(values):
        lanes = values * values
        lanes = jnp.sum(lanes.reshape(EDGE // 8, 8, COLS), axis=0)
        square[...] += lanes

    square[...] = jnp.zeros_like(square)
    own_copy.wait()
    own_id_copy.wait()
    mate_id_copy.wait()
    for copy in mate_copies:
        copy.wait()
    rounds = []
    while 2 ** len(rounds) < n_vocab // 2:
        rounds.append(2 ** len(rounds))

    def tell(k):
        for distance in (rounds[k], n_vocab - rounds[k]):
            pl.semaphore_signal(
                known_sem.at[k], inc=1,
                device_id={"vocab": around(distance), "dp": p}, device_id_type=MESH,
            )

    window_ids = local(jnp.concatenate([own_ids[...], mate_ids[...]], axis=1))
    for block in range(blocks):
        if block < len(rounds):
            tell(block)
        picked = onehot(window_ids, block * EDGE, EDGE)

        @pl.loop(0, chunks)
        def _(chunk):
            here = pl.ds(pl.multiple_of(chunk * COLS, COLS), COLS)
            part = jnp.dot(picked, toks[:, here], preferred_element_type=jnp.float32)
            grad[pl.ds(block * EDGE, EDGE), here] = part
            if 0 < block < blocks - 1:
                add_squares(part)

        if block < len(rounds):
            pl.semaphore_wait(known_sem.at[block], 2)

    for k in range(blocks, len(rounds)):
        tell(k)
        pl.semaphore_wait(known_sem.at[k], 2)

    table_copy.wait()
    halo_pick = []
    for side in range(2):
        for core in range(n_dp):
            remote(
                ids_ref.at[:, pl.ds(0, TOK_EDGE)], halo_ids.at[side, core],
                halo_id_send.at[side, core], halo_id_recv.at[side, core],
                {"vocab": above, "dp": core},
            ).wait_recv()
        ids = local(jnp.concatenate([halo_ids[side, core] for core in range(n_dp)], axis=1))
        base = (rows - EDGE) if side == 0 else 0
        halo_pick.append((base, onehot(ids, base, EDGE)))
    for chunk in range(chunks):
        here = pl.ds(chunk * COLS, COLS)
        for side in range(2):
            for core in range(n_dp):
                remote(
                    grad_ref.at[0, pl.ds(0, TOK_EDGE), pl.ds(0, COLS)],
                    halo.at[side, core, :, here],
                    halo_send.at[side, core, chunk], halo_recv.at[side, core, chunk],
                    {"vocab": above, "dp": core},
                ).wait_recv()
            base, pick = halo_pick[side]
            part = jnp.dot(
                pick, halo[side, :, :, here].reshape(n_dp * TOK_EDGE, COLS),
                preferred_element_type=jnp.float32,
            )
            total = grad[pl.ds(base, EDGE), here] + part
            grad[pl.ds(base, EDGE), here] = total
            add_squares(total)

    lanes = jnp.sum(square[...], axis=0, keepdims=True)
    lanes = functools.reduce(
        jnp.add, [lanes[:, k * 128:(k + 1) * 128] for k in range(COLS // 128)]
    )
    sums[me] = lanes

    def sum_copy(source, slot, target):
        w, core = target
        return remote(
            sums.at[source], sums.at[source], sum_send.at[slot], sum_recv.at[source],
            {"vocab": w, "dp": core},
        )

    @pl.loop(1, n_vocab)
    def _(distance):
        for core in range(n_dp):
            sum_copy(me, distance * n_dp + core, (around(distance), core)).start()

    sum_copy(me, 0, (v, mate)).start()

    for copy in sent:
        copy.wait_send()

    sum_copy(v * n_dp + mate, 0, (v, mate)).wait_recv()

    @pl.loop(1, n_vocab)
    def _(distance):
        w = around(distance)
        for core in range(n_dp):
            sum_copy(w * n_dp + core, 0, (w, core)).wait_recv()

    total = jnp.sum(jnp.sum(sums[...], axis=0), axis=1, keepdims=True)
    rms = jnp.sqrt(total / (n_vocab * rows * width))
    clip_scale = 1.0 / jnp.maximum(1.0, rms / norm_limit)
    norm_ref[0:1, :] = jnp.broadcast_to(step_rate * clip_scale, (1, 128))
    norm_ref[1:2, :] = jnp.broadcast_to(rms, (1, 128))

    sum_copy(me, 0, (v, mate)).wait_send()

    @pl.loop(1, n_vocab)
    def _(distance):
        for core in range(n_dp):
            sum_copy(me, distance * n_dp + core, (around(distance), core)).wait_send()


def update(grad, table, norm_ref, out_ref, rms_ref, outbuf, rms_held, out_sem, rms_sem):
    rms_held[0] = norm_ref[1, 0]
    rms_copy = pltpu.make_async_copy(rms_held, rms_ref, rms_sem)
    rms_copy.start()
    rate = norm_ref[0:1, 0:1]
    stores = []
    for block in range(grad.shape[0] // STORE_ROWS):
        here = pl.ds(block * STORE_ROWS, STORE_ROWS)
        moved = table[here, :].astype(jnp.float32) - rate * grad[here, :]
        outbuf[here, :] = moved.astype(jnp.bfloat16)
        copy = pltpu.make_async_copy(outbuf.at[here, :], out_ref.at[here, :], out_sem.at[block])
        copy.start()
        stores.append(copy)
    for copy in stores:
        copy.wait()
    rms_copy.wait()


def solution(mesh):
    n_vocab, n_dp = mesh.shape["vocab"], mesh.shape["dp"]
    n = n_vocab * n_dp

    def body(embed_table, token_ids, grad_rows):
        rows, width = embed_table.shape
        tokens = token_ids.shape[1]
        half = width // n_dp
        chunks = half // COLS
        in_vmem = pl.BlockSpec(memory_space=pltpu.VMEM)
        in_hbm = pl.BlockSpec(memory_space=pltpu.HBM)
        grad, table, norm = pl.pallas_call(
            functools.partial(kernel, (n_vocab, n_dp)),
            name="clipped_update",
            out_shape=(
                jax.ShapeDtypeStruct((rows, half), jnp.float32),
                jax.ShapeDtypeStruct((rows, half), jnp.bfloat16),
                jax.ShapeDtypeStruct((8, 128), jnp.float32),
            ),
            in_specs=[in_hbm, in_hbm, in_hbm],
            out_specs=(in_vmem, in_vmem, in_vmem),
            scratch_shapes=[
                pltpu.VMEM((n_dp * tokens, half), jnp.bfloat16),
                pltpu.VMEM((2, n_dp, TOK_EDGE, half), jnp.bfloat16),
                pltpu.VMEM((1, tokens), jnp.int32),
                pltpu.VMEM((1, tokens), jnp.int32),
                pltpu.VMEM((2, n_dp, 1, TOK_EDGE), jnp.int32),
                pltpu.VMEM((8, COLS), jnp.float32),
                pltpu.VMEM((n, 1, 128), jnp.float32),
                pltpu.SemaphoreType.DMA,
                pltpu.SemaphoreType.DMA,
                pltpu.SemaphoreType.DMA,
                pltpu.SemaphoreType.DMA((2, chunks)),
                pltpu.SemaphoreType.DMA((2,)),
                pltpu.SemaphoreType.DMA((2, n_dp, chunks)),
                pltpu.SemaphoreType.DMA((2, n_dp, chunks)),
                pltpu.SemaphoreType.DMA((2, n_dp)),
                pltpu.SemaphoreType.DMA((2, n_dp)),
                pltpu.SemaphoreType.DMA((n,)),
                pltpu.SemaphoreType.DMA((n,)),
                pltpu.SemaphoreType.REGULAR((max(n_vocab.bit_length(), 1),)),
            ],
            compiler_params=pltpu.CompilerParams(
                collective_id=0, has_side_effects=True, vmem_limit_bytes=38 * 1024 * 1024
            ),
        )(*(pltpu.with_memory_space_constraint(x, pltpu.HBM) for x in (embed_table, token_ids, grad_rows)))
        updated, grad_rms = pl.pallas_call(
            update,
            name="clipped_step",
            out_shape=(
                jax.ShapeDtypeStruct((rows, half), jnp.bfloat16),
                jax.ShapeDtypeStruct((1,), jnp.float32),
            ),
            in_specs=[in_vmem, in_vmem, in_vmem],
            out_specs=(in_hbm, in_hbm),
            scratch_shapes=[
                pltpu.VMEM((rows, half), jnp.bfloat16),
                pltpu.SMEM((1,), jnp.float32),
                pltpu.SemaphoreType.DMA((rows // STORE_ROWS,)),
                pltpu.SemaphoreType.DMA,
            ],
            compiler_params=pltpu.CompilerParams(vmem_limit_bytes=24 * 1024 * 1024),
        )(grad, table, norm)
        return updated, grad_rms

    in_specs = (P("vocab", None), P("dp", "vocab"), P("dp", "vocab", None))
    out_specs = (P("vocab", "dp"), P())
    return jax.shard_map(body, mesh=mesh, in_specs=in_specs, out_specs=out_specs, check_vma=False)
```

profile of v0, /device:TPU:0, one launch (start us, length us, event | category | flops | bytes accessed | tf_op | source)
XLA Modules:
  0.0 61.1 jit_solution(3139395482067051504)
XLA Ops:
  0.6 57.8 %clipped_update.1 = (f32[1024,2048]{1,0:T(8,128)S(1)}, bf16[1024,2048]{1,0:T(8,128)(2,1)S(1)}, f32[8,128]{1,0:T(8,128)S(1)}) custom-call(bf16[1024,4096]{1,0:T(8,128)(2,1)} %table_ref.1, s32[1,1024]{1,0:T(1,128)} %ids_ref.1, bf16[1,1024,4096]{2,1,0:T(8,128)(2,1)} %grad_ref.1), custom_call_target="tpu_custom_call" | custom-call | tf_op jit(solution)/shard_map/clipped_update/pallas_call | solution.py:263
  58.4 2.7 %clipped_step.1 = (bf16[1024,2048]{1,0:T(8,128)(2,1)}, f32[1]{0:T(128)}) custom-call(f32[1024,2048]{1,0:T(8,128)S(1)} %get-tuple-element.5.grad, bf16[1024,2048]{1,0:T(8,128)(2,1)S(1)} %get-tuple-element.6.table, f32[8,128]{1,0:T(8,128)S(1)} %get-tuple-element.7.norm_ref), custom_call_target="tpu_custom_call" | custom-call | tf_op jit(solution)/shard_map/clipped_step/pallas_call | solution.py:298
where the time goes:
time: 61.3 us; the launch traced here: 61.1 us
  Pallas kernels  60.5 us (99%)
  between operations  0.64 us (1%)
    pallas_call x1, Pallas kernels, body(): pl.pallas_call(functools.partial(kernel, (n_vocab, n_dp)), name='clipped_...  57.8 us
    pallas_call x1, Pallas kernels, body(): pl.pallas_call(update, name='clipped_step', out_shape=(jax.ShapeDtypeStru...  2.69 us

commit v1 on v0

v1 whole, which is shorter than its diff:
```python
import functools

import jax
import jax.numpy as jnp
from jax import lax
from jax.experimental import pallas as pl
from jax.experimental.pallas import tpu as pltpu
from jax.sharding import PartitionSpec as P

MESH = pl.DeviceIdType.MESH
TOK_EDGE = 128
EDGE = 256
COLS = 512
STORE_ROWS = 32

step_rate = 0.5
norm_limit = 1.0


def chunk_plan(half):
    quarter = half // 4
    narrow = 128
    return (
        (0, 0, quarter),
        (1, 0, 2 * quarter),
        (1, 2 * quarter, 2 * quarter),
        (0, quarter, quarter),
        (0, 2 * quarter, quarter),
        (0, 3 * quarter, quarter - narrow),
        (0, half - narrow, narrow),
    )


def kernel(sizes, table_ref, ids_ref, grad_ref, grad, table, norm_ref,
           toks, halo, stage, own_ids, mate_ids, halo_ids, square, sums,
           own_sem, own_id_sem, table_sem, stage_sem, mate_sem, mate_id_sem,
           halo_send, halo_recv, halo_id_send, halo_id_recv, sum_send, sum_recv, known_sem):
    n_vocab, n_dp = sizes
    rows, width = table_ref.shape
    tokens = ids_ref.shape[1]
    half = width // n_dp
    n = n_vocab * n_dp
    blocks = rows // EDGE
    bits = n_vocab.bit_length() - 1
    plan = chunk_plan(half)
    v = lax.axis_index("vocab")
    p = lax.axis_index("dp")
    me = v * n_dp + p
    mate = 1 - p
    odd = lax.rem(v, 2)
    below = lax.rem(v + n_vocab - 1, n_vocab)
    above = lax.rem(v + 1, n_vocab)
    steps = [(1 << k) - 2 * (1 << k) * lax.rem(v // (1 << k), 2) for k in range(bits)]

    def across(mask):
        return functools.reduce(lambda a, b: a + b, [steps[k] for k in range(bits) if mask >> k & 1], v)

    partner = across(1)
    far = jnp.where(odd == 1, above, below)
    last = tokens - TOK_EDGE
    targets = (partner, far)
    firsts = tuple(
        pl.multiple_of(first, TOK_EDGE) for first in ((1 - odd) * last, odd * last)
    )
    bases = tuple(
        pl.multiple_of(base, EDGE) for base in ((1 - odd) * (rows - EDGE), odd * (rows - EDGE))
    )

    def columns(core, start, count):
        return pl.ds(pl.multiple_of(core * half + start, 128), count)

    def remote(src, dst, send, recv, device):
        return pltpu.make_async_remote_copy(
            src_ref=src, dst_ref=dst, send_sem=send, recv_sem=recv,
            device_id={"vocab": device[0], "dp": device[1]}, device_id_type=MESH,
        )

    stage_copies = [
        pltpu.make_async_copy(
            grad_ref.at[0, pl.ds(firsts[0], TOK_EDGE), pl.ds(core * half, plan[0][2])],
            stage.at[core], stage_sem.at[core],
        )
        for core in range(n_dp)
    ]
    for copy in stage_copies:
        copy.start()
    barrier = pltpu.get_barrier_semaphore()
    greeted = [(partner, core) for core in range(n_dp)] + [(v, mate)]
    greeted += [(across(1 << k), p) for k in range(1, bits)]
    for w, core in greeted:
        pl.semaphore_signal(
            barrier, inc=1, device_id={"vocab": w, "dp": core}, device_id_type=MESH
        )
    own_half = pl.ds(pl.multiple_of(p * half, half), half)
    own_copy = pltpu.make_async_copy(
        grad_ref.at[0, :, own_half], toks.at[pl.ds(0, tokens), :], own_sem
    )
    own_copy.start()
    own_id_copy = pltpu.make_async_copy(ids_ref, own_ids, own_id_sem)
    own_id_copy.start()
    table_copy = pltpu.make_async_copy(table_ref.at[:, own_half], table, table_sem)
    for copy in stage_copies:
        copy.wait()
    pl.semaphore_wait(barrier, len(greeted))

    def send_chunk(at):
        k, start, count = plan[at]
        for core in range(n_dp):
            src = stage.at[core] if at == 0 else grad_ref.at[
                0, pl.ds(firsts[k], TOK_EDGE), pl.ds(core * half + start, count)
            ]
            remote(
                src, halo.at[k, p, :, pl.ds(start, count)],
                halo_send, halo_recv.at[at], (targets[k], core),
            ).start()

    def send_ids(k):
        for core in range(n_dp):
            remote(
                ids_ref.at[:, pl.ds(firsts[k], TOK_EDGE)], halo_ids.at[k, p],
                halo_id_send, halo_id_recv, (targets[k], core),
            ).start()

    send_chunk(0)
    for k in range(1, bits):
        pl.semaphore_signal(
            known_sem.at[k - 1], inc=1,
            device_id={"vocab": across(1 << k), "dp": p}, device_id_type=MESH,
        )
        if k == 1:
            mate_copy = remote(
                grad_ref.at[0, :, columns(mate, 0, half)], toks.at[pl.ds(tokens, tokens), :],
                mate_sem.at[0], mate_sem.at[1], (v, mate),
            )
            mate_copy.start()
            mate_id_copy = remote(
                ids_ref, mate_ids, mate_id_sem.at[0], mate_id_sem.at[1], (v, mate)
            )
            mate_id_copy.start()
            send_ids(0)
            table_copy.start()
        pl.semaphore_wait(known_sem.at[k - 1], 1)
    send_ids(1)
    for at in range(1, len(plan)):
        send_chunk(at)

    own_start = v * rows

    def local(ids):
        shifted = ids - own_start
        return jnp.where(shifted < 0, shifted + n_vocab * rows, shifted)

    def onehot(ids, base, count):
        index = lax.broadcasted_iota(jnp.int32, (count, ids.shape[1]), 0) + base
        return jnp.where(ids == index, 1.0, 0.0).astype(jnp.bfloat16)

    def add_squares(values):
        count, wide = values.shape
        lanes = jnp.sum((values * values).reshape(count // 8, 8, wide), axis=0)
        square[...] += functools.reduce(
            jnp.add, [lanes[:, i * 128:(i + 1) * 128] for i in range(wide // 128)]
        )

    square[...] = jnp.zeros_like(square)
    own_id_copy.wait()
    mate_id_copy.wait()
    own_copy.wait()
    mate_copy.wait()

    window_ids = local(jnp.concatenate([own_ids[...], mate_ids[...]], axis=1))
    for block in range(blocks):
        picked = onehot(window_ids, block * EDGE, EDGE)

        @pl.loop(0, half // COLS)
        def _(chunk):
            here = pl.ds(pl.multiple_of(chunk * COLS, COLS), COLS)
            part = jnp.dot(picked, toks[:, here], preferred_element_type=jnp.float32)
            grad[pl.ds(block * EDGE, EDGE), here] = part
            if 0 < block < blocks - 1:
                add_squares(part)

    remote(
        halo_ids, halo_ids, halo_id_send, halo_id_recv, (partner, p)
    ).wait_recv()
    picks = []
    for k in range(2):
        ids = local(jnp.concatenate([halo_ids[k, core] for core in range(n_dp)], axis=1))
        picks.append(onehot(ids, bases[k], EDGE))
    table_copy.wait()
    for at, (k, start, count) in enumerate(plan):
        here = pl.ds(start, count)
        arrived = halo.at[k, :, :, here]
        remote(arrived, arrived, halo_send, halo_recv.at[at], (partner, p)).wait_recv()
        part = jnp.dot(
            picks[k], halo[k, :, :, here].reshape(n_dp * TOK_EDGE, count),
            preferred_element_type=jnp.float32,
        )
        total = grad[pl.ds(bases[k], EDGE), here] + part
        grad[pl.ds(bases[k], EDGE), here] = total
        add_squares(total)

    sums[me] = jnp.sum(square[...], axis=0, keepdims=True)
    for mask in range(n_vocab - 1, -1, -1):
        for core in (mate, p):
            if mask or core is mate:
                remote(
                    sums.at[me], sums.at[me], sum_send, sum_recv, (across(mask), core)
                ).start()
    remote(halo, halo, halo_send, halo_recv.at[0], (partner, p)).wait_send()
    remote(halo_ids, halo_ids, halo_id_send, halo_id_recv, (partner, p)).wait_send()
    others = sums.at[pl.ds(0, n - 1)]
    all_sums = remote(others, others, sum_send, sum_recv, (partner, p))
    all_sums.wait_recv()

    total = jnp.sum(jnp.sum(sums[...], axis=0), axis=1, keepdims=True)
    rms = jnp.sqrt(total / (n_vocab * rows * width))
    clip_scale = 1.0 / jnp.maximum(1.0, rms / norm_limit)
    norm_ref[0:1, :] = jnp.broadcast_to(step_rate * clip_scale, (1, 128))
    norm_ref[1:2, :] = jnp.broadcast_to(rms, (1, 128))
    all_sums.wait_send()


def update(grad, table, norm_ref, out_ref, rms_ref, outbuf, rms_held, out_sem, rms_sem):
    rms_held[0] = norm_ref[1, 0]
    rms_copy = pltpu.make_async_copy(rms_held, rms_ref, rms_sem)
    rms_copy.start()
    rate = norm_ref[0:1, 0:1]
    for block in range(grad.shape[0] // STORE_ROWS):
        here = pl.ds(block * STORE_ROWS, STORE_ROWS)
        moved = table[here, :].astype(jnp.float32) - rate * grad[here, :]
        outbuf[here, :] = moved.astype(jnp.bfloat16)
        pltpu.make_async_copy(outbuf.at[here, :], out_ref.at[here, :], out_sem).start()
    pltpu.make_async_copy(outbuf, out_ref, out_sem).wait()
    rms_copy.wait()


def solution(mesh):
    n_vocab, n_dp = mesh.shape["vocab"], mesh.shape["dp"]
    n = n_vocab * n_dp
    bits = n_vocab.bit_length() - 1

    def body(embed_table, token_ids, grad_rows):
        rows, width = embed_table.shape
        tokens = token_ids.shape[1]
        half = width // n_dp
        plan = chunk_plan(half)
        in_vmem = pl.BlockSpec(memory_space=pltpu.VMEM)
        in_hbm = pl.BlockSpec(memory_space=pltpu.HBM)
        grad, table, norm = pl.pallas_call(
            functools.partial(kernel, (n_vocab, n_dp)),
            name="clipped_update",
            out_shape=(
                jax.ShapeDtypeStruct((rows, half), jnp.float32),
                jax.ShapeDtypeStruct((rows, half), jnp.bfloat16),
                jax.ShapeDtypeStruct((8, 128), jnp.float32),
            ),
            in_specs=[in_hbm, in_hbm, in_hbm],
            out_specs=(in_vmem, in_vmem, in_vmem),
            scratch_shapes=[
                pltpu.VMEM((n_dp * tokens, half), jnp.bfloat16),
                pltpu.VMEM((2, n_dp, TOK_EDGE, half), jnp.bfloat16),
                pltpu.VMEM((n_dp, TOK_EDGE, plan[0][2]), jnp.bfloat16),
                pltpu.VMEM((1, tokens), jnp.int32),
                pltpu.VMEM((1, tokens), jnp.int32),
                pltpu.VMEM((2, n_dp, 1, TOK_EDGE), jnp.int32),
                pltpu.VMEM((8, 128), jnp.float32),
                pltpu.VMEM((n, 1, 128), jnp.float32),
                pltpu.SemaphoreType.DMA,
                pltpu.SemaphoreType.DMA,
                pltpu.SemaphoreType.DMA,
                pltpu.SemaphoreType.DMA((n_dp,)),
                pltpu.SemaphoreType.DMA((2,)),
                pltpu.SemaphoreType.DMA((2,)),
                pltpu.SemaphoreType.DMA,
                pltpu.SemaphoreType.DMA((len(plan),)),
                pltpu.SemaphoreType.DMA,
                pltpu.SemaphoreType.DMA,
                pltpu.SemaphoreType.DMA,
                pltpu.SemaphoreType.DMA,
                pltpu.SemaphoreType.REGULAR((max(bits - 1, 1),)),
            ],
            compiler_params=pltpu.CompilerParams(
                collective_id=0, has_side_effects=True, vmem_limit_bytes=40 * 1024 * 1024
            ),
        )(*(pltpu.with_memory_space_constraint(x, pltpu.HBM) for x in (embed_table, token_ids, grad_rows)))
        updated, grad_rms = pl.pallas_call(
            update,
            name="clipped_step",
            out_shape=(
                jax.ShapeDtypeStruct((rows, half), jnp.bfloat16),
                jax.ShapeDtypeStruct((1,), jnp.float32),
            ),
            in_specs=[in_vmem, in_vmem, in_vmem],
            out_specs=(in_hbm, in_hbm),
            scratch_shapes=[
                pltpu.VMEM((rows, half), jnp.bfloat16),
                pltpu.SMEM((1,), jnp.float32),
                pltpu.SemaphoreType.DMA,
                pltpu.SemaphoreType.DMA,
            ],
            compiler_params=pltpu.CompilerParams(vmem_limit_bytes=24 * 1024 * 1024),
        )(grad, table, norm)
        return updated, grad_rms

    in_specs = (P("vocab", None), P("dp", "vocab"), P("dp", "vocab", None))
    out_specs = (P("vocab", "dp"), P())
    return jax.shard_map(body, mesh=mesh, in_specs=in_specs, out_specs=out_specs, check_vma=False)
```

time: 61.3 us -> 59.7 us (0.974)
  Pallas kernels: 60.5 us -> 58.9 us
    pallas_call x1, Pallas kernels: 57.8 us -> 56.7 us  [body(): pl.pallas_call(functools.partial(kernel, (n_vocab, n_dp)), name='clipped_...]
where the time goes in v1:
time: 59.7 us; the launch traced here: 59.6 us
  Pallas kernels  58.9 us (99%)
  between operations  0.64 us (1%)
    pallas_call x1, Pallas kernels, body(): pl.pallas_call(functools.partial(kernel, (n_vocab, n_dp)), name='clipped_...  56.7 us
    pallas_call x1, Pallas kernels, body(): pl.pallas_call(update, name='clipped_step', out_shape=(jax.ShapeDtypeStru...  2.21 us

profile of v1, /device:TPU:0, one launch (start us, length us, event | category | flops | bytes accessed | tf_op | source)
XLA Modules:
  0.0 59.6 jit_solution(4749754041374953562)
XLA Ops:
  0.6 56.7 %clipped_update.1 = (f32[1024,2048]{1,0:T(8,128)S(1)}, bf16[1024,2048]{1,0:T(8,128)(2,1)S(1)}, f32[8,128]{1,0:T(8,128)S(1)}) custom-call(bf16[1024,4096]{1,0:T(8,128)(2,1)} %table_ref.1, s32[1,1024]{1,0:T(1,128)} %ids_ref.1, bf16[1,1024,4096]{2,1,0:T(8,128)(2,1)} %grad_ref.1), custom_call_target="tpu_custom_call" | custom-call | tf_op jit(solution)/shard_map/clipped_update/pallas_call | solution.py:249
  57.4 2.2 %clipped_step.1 = (bf16[1024,2048]{1,0:T(8,128)(2,1)}, f32[1]{0:T(128)}) custom-call(f32[1024,2048]{1,0:T(8,128)S(1)} %get-tuple-element.5.grad, bf16[1024,2048]{1,0:T(8,128)(2,1)S(1)} %get-tuple-element.6.table, f32[8,128]{1,0:T(8,128)S(1)} %get-tuple-element.7.norm_ref), custom_call_target="tpu_custom_call" | custom-call | tf_op jit(solution)/shard_map/clipped_step/pallas_call | solution.py:286

commit v2 on v1

--- a/solution.py
+++ b/solution.py
@@ -11,10 +11,15 @@
 TOK_EDGE = 128
 EDGE = 256
 COLS = 512
-STORE_ROWS = 32
+STORE_ROWS = 16
+STORE_COLS = 256
 
 step_rate = 0.5
 norm_limit = 1.0
+
+
+RELAYED = ((4, 0), (4, 1))
+RELAY_FROM = (2, 3)
 
 
 def chunk_plan(half):
@@ -22,9 +27,11 @@
     narrow = 128
     return (
         (0, 0, quarter),
+        (0, quarter, 2 * narrow),
         (1, 0, 2 * quarter),
         (1, 2 * quarter, 2 * quarter),
-        (0, quarter, quarter),
+        (0, quarter + 2 * narrow, narrow),
+        (0, quarter + 3 * narrow, narrow),
         (0, 2 * quarter, quarter),
         (0, 3 * quarter, quarter - narrow),
         (0, half - narrow, narrow),
@@ -32,9 +39,10 @@
 
 
 def kernel(sizes, table_ref, ids_ref, grad_ref, grad, table, norm_ref,
-           toks, halo, stage, own_ids, mate_ids, halo_ids, square, sums,
+           toks, halo, stage, relayed, own_ids, mate_ids, halo_ids, square, sums,
            own_sem, own_id_sem, table_sem, stage_sem, mate_sem, mate_id_sem,
-           halo_send, halo_recv, halo_id_send, halo_id_recv, sum_send, sum_recv, known_sem):
+           halo_send, halo_recv, halo_id_send, halo_id_recv, sum_send, sum_recv,
+           relay_send, relay_recv, known_sem):
     n_vocab, n_dp = sizes
     rows, width = table_ref.shape
     tokens = ids_ref.shape[1]
@@ -50,12 +58,16 @@
     odd = lax.rem(v, 2)
     below = lax.rem(v + n_vocab - 1, n_vocab)
     above = lax.rem(v + 1, n_vocab)
-    steps = [(1 << k) - 2 * (1 << k) * lax.rem(v // (1 << k), 2) for k in range(bits)]
+    set_bits = [lax.rem(v // (1 << k), 2) for k in range(bits)]
+    steps = [(1 << k) - 2 * (1 << k) * set_bits[k] for k in range(bits)]
+    zone = v // (n_vocab // 4)
 
     def across(mask):
         return functools.reduce(lambda a, b: a + b, [steps[k] for k in range(bits) if mask >> k & 1], v)
 
     partner = across(1)
+    opposite = across(3 * n_vocab // 4)
+    beyond = across(3 * n_vocab // 4 + 1)
     far = jnp.where(odd == 1, above, below)
     last = tokens - TOK_EDGE
     targets = (partner, far)
@@ -85,12 +97,20 @@
     for copy in stage_copies:
         copy.start()
     barrier = pltpu.get_barrier_semaphore()
-    greeted = [(partner, core) for core in range(n_dp)] + [(v, mate)]
-    greeted += [(across(1 << k), p) for k in range(1, bits)]
-    for w, core in greeted:
+
+    def greet(w, core):
         pl.semaphore_signal(
             barrier, inc=1, device_id={"vocab": w, "dp": core}, device_id_type=MESH
         )
+
+    for core in range(n_dp):
+        greet(partner, core)
+    greet(v, mate)
+    greet(across(2), p)
+    for k in range(2, bits):
+        pl.when(set_bits[k] == 0)(functools.partial(greet, across(1 << k), p))
+    pl.when(zone < 2)(functools.partial(greet, beyond, p))
+    awaited = n_dp + 2 + sum(set_bits[2:]) + zone // 2
     own_half = pl.ds(pl.multiple_of(p * half, half), half)
     own_copy = pltpu.make_async_copy(
         grad_ref.at[0, :, own_half], toks.at[pl.ds(0, tokens), :], own_sem
@@ -101,18 +121,32 @@
     table_copy = pltpu.make_async_copy(table_ref.at[:, own_half], table, table_sem)
     for copy in stage_copies:
         copy.wait()
-    pl.semaphore_wait(barrier, len(greeted))
+    pl.semaphore_wait(barrier, awaited)
+
+    def source(at, core):
+        k, start, count = plan[at]
+        return grad_ref.at[0, pl.ds(firsts[k], TOK_EDGE), pl.ds(core * half + start, count)]
+
+    def place(at):
+        k, start, count = plan[at]
+        return halo.at[k, p, :, pl.ds(start, count)]
 
     def send_chunk(at):
-        k, start, count = plan[at]
         for core in range(n_dp):
-            src = stage.at[core] if at == 0 else grad_ref.at[
-                0, pl.ds(firsts[k], TOK_EDGE), pl.ds(core * half + start, count)
-            ]
-            remote(
-                src, halo.at[k, p, :, pl.ds(start, count)],
-                halo_send, halo_recv.at[at], (targets[k], core),
-            ).start()
+            copy = remote(
+                stage.at[core] if at == 0 else source(at, core), place(at),
+                halo_send, halo_recv.at[at], (targets[plan[at][0]], core),
+            )
+            if (at, core) in RELAYED:
+                pl.when(zone < RELAY_FROM[RELAYED.index((at, core))])(copy.start)
+            else:
+                copy.start()
+
+    def relay_units(count):
+        return remote(
+            relayed.at[pl.ds(0, count)], relayed.at[pl.ds(0, count)],
+            relay_send, relay_recv, (opposite, p),
+        )
 
     def send_ids(k):
         for core in range(n_dp):
@@ -121,27 +155,54 @@
                 halo_id_send, halo_id_recv, (targets[k], core),
             ).start()
 
+    for unit, (at, core) in enumerate(RELAYED):
+        copy = remote(
+            source(at, core), relayed.at[unit], halo_send, relay_recv, (beyond, p)
+        )
+        pl.when(zone >= RELAY_FROM[unit])(copy.start)
     send_chunk(0)
-    for k in range(1, bits):
+    send_chunk(1)
+    mate_copy = remote(
+        grad_ref.at[0, :, columns(mate, 0, half)], toks.at[pl.ds(tokens, tokens), :],
+        mate_sem.at[0], mate_sem.at[1], (v, mate),
+    )
+    mate_copy.start()
+    mate_id_copy = remote(
+        ids_ref, mate_ids, mate_id_sem.at[0], mate_id_sem.at[1], (v, mate)
+    )
+    mate_id_copy.start()
+    send_ids(0)
+    table_copy.start()
+
+    def tell(k):
         pl.semaphore_signal(
             known_sem.at[k - 1], inc=1,
             device_id={"vocab": across(1 << k), "dp": p}, device_id_type=MESH,
         )
+
+    for k in range(1, bits):
         if k == 1:
-            mate_copy = remote(
-                grad_ref.at[0, :, columns(mate, 0, half)], toks.at[pl.ds(tokens, tokens), :],
-                mate_sem.at[0], mate_sem.at[1], (v, mate),
-            )
-            mate_copy.start()
-            mate_id_copy = remote(
-                ids_ref, mate_ids, mate_id_sem.at[0], mate_id_sem.at[1], (v, mate)
-            )
-            mate_id_copy.start()
-            send_ids(0)
-            table_copy.start()
+            tell(k)
+        else:
+            pl.when(set_bits[k] == 1)(functools.partial(tell, k))
         pl.semaphore_wait(known_sem.at[k - 1], 1)
+        if k > 1:
+            pl.when(set_bits[k] == 0)(functools.partial(tell, k))
     send_ids(1)
-    for at in range(1, len(plan)):
+
+    for owner in range(2):
+        units = [unit for unit in range(len(RELAYED)) if RELAY_FROM[unit] <= 3 - owner]
+
+        @pl.when(zone == owner)
+        def _():
+            relay_units(len(units)).wait_recv()
+            for unit in units:
+                at, core = RELAYED[unit]
+                remote(
+                    relayed.at[unit], place(at), relay_send, halo_recv.at[at], (opposite, core)
+                ).start()
+
+    for at in range(2, len(plan)):
         send_chunk(at)
 
     own_start = v * rows
@@ -179,9 +240,7 @@
             if 0 < block < blocks - 1:
                 add_squares(part)
 
-    remote(
-        halo_ids, halo_ids, halo_id_send, halo_id_recv, (partner, p)
-    ).wait_recv()
+    remote(halo_ids, halo_ids, halo_id_send, halo_id_recv, (partner, p)).wait_recv()
     picks = []
     for k in range(2):
         ids = local(jnp.concatenate([halo_ids[k, core] for core in range(n_dp)], axis=1))
@@ -200,14 +259,15 @@
         add_squares(total)
 
     sums[me] = jnp.sum(square[...], axis=0, keepdims=True)
-    for mask in range(n_vocab - 1, -1, -1):
-        for core in (mate, p):
-            if mask or core is mate:
-                remote(
-                    sums.at[me], sums.at[me], sum_send, sum_recv, (across(mask), core)
-                ).start()
+    for w in range(n_vocab):
+        for core in range(n_dp):
+            copy = remote(sums.at[me], sums.at[me], sum_send, sum_recv, (w, core))
+            pl.when(me != w * n_dp + core)(copy.start)
     remote(halo, halo, halo_send, halo_recv.at[0], (partner, p)).wait_send()
     remote(halo_ids, halo_ids, halo_id_send, halo_id_recv, (partner, p)).wait_send()
+    for owner in range(2):
+        count = sum(start <= 3 - owner for start in RELAY_FROM)
+        pl.when(zone == owner)(relay_units(count).wait_send)
     others = sums.at[pl.ds(0, n - 1)]
     all_sums = remote(others, others, sum_send, sum_recv, (partner, p))
     all_sums.wait_recv()
@@ -227,8 +287,10 @@
     rate = norm_ref[0:1, 0:1]
     for block in range(grad.shape[0] // STORE_ROWS):
         here = pl.ds(block * STORE_ROWS, STORE_ROWS)
-        moved = table[here, :].astype(jnp.float32) - rate * grad[here, :]
-        outbuf[here, :] = moved.astype(jnp.bfloat16)
+        for start in range(0, grad.shape[1], STORE_COLS):
+            at = (here, pl.ds(start, STORE_COLS))
+            moved = table[at].astype(jnp.float32) - rate * grad[at]
+            outbuf[at] = moved.astype(jnp.bfloat16)
         pltpu.make_async_copy(outbuf.at[here, :], out_ref.at[here, :], out_sem).start()
     pltpu.make_async_copy(outbuf, out_ref, out_sem).wait()
     rms_copy.wait()
@@ -260,6 +322,7 @@
                 pltpu.VMEM((n_dp * tokens, half), jnp.bfloat16),
                 pltpu.VMEM((2, n_dp, TOK_EDGE, half), jnp.bfloat16),
                 pltpu.VMEM((n_dp, TOK_EDGE, plan[0][2]), jnp.bfloat16),
+                pltpu.VMEM((len(RELAYED), TOK_EDGE, plan[RELAYED[0][0]][2]), jnp.bfloat16),
                 pltpu.VMEM((1, tokens), jnp.int32),
                 pltpu.VMEM((1, tokens), jnp.int32),
                 pltpu.VMEM((2, n_dp, 1, TOK_EDGE), jnp.int32),
@@ -273,6 +336,8 @@
                 pltpu.SemaphoreType.DMA((2,)),
                 pltpu.SemaphoreType.DMA,
                 pltpu.SemaphoreType.DMA((len(plan),)),
+                pltpu.SemaphoreType.DMA,
+                pltpu.SemaphoreType.DMA,
                 pltpu.SemaphoreType.DMA,
                 pltpu.SemaphoreType.DMA,
                 pltpu.SemaphoreType.DMA,

time: 59.7 us -> 58.3 us (0.977)
  Pallas kernels: 58.9 us -> 57.5 us
    pallas_call x1, Pallas kernels: 56.7 us -> 55.4 us  [body(): pl.pallas_call(functools.partial(kernel, (n_vocab, n_dp)), name='clipped_...]
where the time goes in v2:
time: 58.3 us; the launch traced here: 58.1 us
  Pallas kernels  57.5 us (99%)
  between operations  0.64 us (1%)
    pallas_call x1, Pallas kernels, body(): pl.pallas_call(functools.partial(kernel, (n_vocab, n_dp)), name='clipped_...  55.4 us
    pallas_call x1, Pallas kernels, body(): pl.pallas_call(update, name='clipped_step', out_shape=(jax.ShapeDtypeStru...  2.03 us

profile of v2, /device:TPU:0, one launch (start us, length us, event | category | flops | bytes accessed | tf_op | source)
XLA Modules:
  0.0 58.1 jit_solution(11456214679223753499)
XLA Ops:
  0.6 55.4 %clipped_update.1 = (f32[1024,2048]{1,0:T(8,128)S(1)}, bf16[1024,2048]{1,0:T(8,128)(2,1)S(1)}, f32[8,128]{1,0:T(8,128)S(1)}) custom-call(bf16[1024,4096]{1,0:T(8,128)(2,1)} %table_ref.1, s32[1,1024]{1,0:T(1,128)} %ids_ref.1, bf16[1,1024,4096]{2,1,0:T(8,128)(2,1)} %grad_ref.1), custom_call_target="tpu_custom_call" | custom-call | tf_op jit(solution)/shard_map/clipped_update/pallas_call | solution.py:311
  56.1 2.0 %clipped_step.1 = (bf16[1024,2048]{1,0:T(8,128)(2,1)}, f32[1]{0:T(128)}) custom-call(f32[1024,2048]{1,0:T(8,128)S(1)} %get-tuple-element.5.grad, bf16[1024,2048]{1,0:T(8,128)(2,1)S(1)} %get-tuple-element.6.table, f32[8,128]{1,0:T(8,128)S(1)} %get-tuple-element.7.norm_ref), custom_call_target="tpu_custom_call" | custom-call | tf_op jit(solution)/shard_map/clipped_step/pallas_call | solution.py:351

commit v3 on v2

--- a/solution.py
+++ b/solution.py
@@ -18,31 +18,50 @@
 norm_limit = 1.0
 
 
-RELAYED = ((4, 0), (4, 1))
-RELAY_FROM = (2, 3)
+PIECE = 512
+
+RELAYED = {
+    (2, 0, 0): ((0, 3, 0),),
+    (2, 1, 0): ((0, 3, 0),),
+    (3, 0, 0): ((0, 3, 0), (1, 3, 1)),
+    (3, 0, 1): ((0, 3, 0), (1, 3, 1)),
+    (3, 1, 0): ((0, 3, 0), (1, 3, 1)),
+    (3, 1, 1): ((0, 3, 0), (1, 3, 1)),
+}
+SLOTS = 2
+FAR_NARROW = 8
+FAR_RELAYED = {(0, 0): 1, (0, 1): 1, (1, 0): 1, (1, 1): 1, (2, 0): 1, (3, 0): 1}
 
 
 def chunk_plan(half):
     quarter = half // 4
     narrow = 128
     return (
-        (0, 0, quarter),
-        (0, quarter, 2 * narrow),
-        (1, 0, 2 * quarter),
-        (1, 2 * quarter, 2 * quarter),
-        (0, quarter + 2 * narrow, narrow),
-        (0, quarter + 3 * narrow, narrow),
-        (0, 2 * quarter, quarter),
-        (0, 3 * quarter, quarter - narrow),
-        (0, half - narrow, narrow),
-    )
+        (0, 0, quarter, 0),
+        (0, quarter, 2 * narrow, 0),
+        (1, 0, half - narrow, 1),
+        (0, quarter + 2 * narrow, narrow, 2),
+        (0, quarter + 3 * narrow, narrow, 3),
+        (0, 2 * quarter, quarter, 4),
+        (0, 3 * quarter, quarter - narrow, 5),
+        (0, half - narrow, narrow, 7),
+        (1, half - narrow, narrow, 6),
+    )
+
+
+def groups_of(plan):
+    groups = {}
+    for k, start, count, group in plan:
+        first = groups.get(group, (k, start, 0))
+        groups[group] = (k, first[1], first[2] + count)
+    return [groups[group] for group in sorted(groups)]
 
 
 def kernel(sizes, table_ref, ids_ref, grad_ref, grad, table, norm_ref,
            toks, halo, stage, relayed, own_ids, mate_ids, halo_ids, square, sums,
            own_sem, own_id_sem, table_sem, stage_sem, mate_sem, mate_id_sem,
            halo_send, halo_recv, halo_id_send, halo_id_recv, sum_send, sum_recv,
-           relay_send, relay_recv, known_sem):
+           relay_send, relay_recv, far_send, far_recv, known_sem):
     n_vocab, n_dp = sizes
     rows, width = table_ref.shape
     tokens = ids_ref.shape[1]
@@ -61,13 +80,12 @@
     set_bits = [lax.rem(v // (1 << k), 2) for k in range(bits)]
     steps = [(1 << k) - 2 * (1 << k) * set_bits[k] for k in range(bits)]
     zone = v // (n_vocab // 4)
+    top = 3 * n_vocab // 4
 
     def across(mask):
         return functools.reduce(lambda a, b: a + b, [steps[k] for k in range(bits) if mask >> k & 1], v)
 
     partner = across(1)
-    opposite = across(3 * n_vocab // 4)
-    beyond = across(3 * n_vocab // 4 + 1)
     far = jnp.where(odd == 1, above, below)
     last = tokens - TOK_EDGE
     targets = (partner, far)
@@ -87,30 +105,40 @@
             device_id={"vocab": device[0], "dp": device[1]}, device_id_type=MESH,
         )
 
+    barrier = pltpu.get_barrier_semaphore()
+
+    def greet(w, core):
+        pl.semaphore_signal(
+            barrier, inc=1, device_id={"vocab": w, "dp": core}, device_id_type=MESH
+        )
+
+    def at_place(quarter, second, core=None):
+        here = jnp.logical_and(zone == quarter, set_bits[1] == second)
+        return here if core is None else jnp.logical_and(here, p == core)
+
+    relay = across(top + 1)
+    beyond = across(top)
+    via = far + jnp.where(odd == 1, 1, -1)
+    far_quarter = far // (n_vocab // 4)
+
+    for core in range(n_dp):
+        greet(partner, core)
+    greet(v, mate)
     stage_copies = [
         pltpu.make_async_copy(
             grad_ref.at[0, pl.ds(firsts[0], TOK_EDGE), pl.ds(core * half, plan[0][2])],
-            stage.at[core], stage_sem.at[core],
+            stage.at[core], stage_sem,
         )
         for core in range(n_dp)
     ]
     for copy in stage_copies:
         copy.start()
-    barrier = pltpu.get_barrier_semaphore()
-
-    def greet(w, core):
-        pl.semaphore_signal(
-            barrier, inc=1, device_id={"vocab": w, "dp": core}, device_id_type=MESH
-        )
-
-    for core in range(n_dp):
-        greet(partner, core)
-    greet(v, mate)
-    greet(across(2), p)
-    for k in range(2, bits):
+    for k in range(1, bits):
         pl.when(set_bits[k] == 0)(functools.partial(greet, across(1 << k), p))
-    pl.when(zone < 2)(functools.partial(greet, beyond, p))
-    awaited = n_dp + 2 + sum(set_bits[2:]) + zone // 2
+    awaited = n_dp + 1 + sum(set_bits[1:])
+    for quarter, second in sorted({key[:2] for key in RELAYED}):
+        pl.when(at_place(3 - quarter, second))(functools.partial(greet, relay, p))
+        awaited += at_place(quarter, second).astype(jnp.int32)
     own_half = pl.ds(pl.multiple_of(p * half, half), half)
     own_copy = pltpu.make_async_copy(
         grad_ref.at[0, :, own_half], toks.at[pl.ds(0, tokens), :], own_sem
@@ -119,34 +147,42 @@
     own_id_copy = pltpu.make_async_copy(ids_ref, own_ids, own_id_sem)
     own_id_copy.start()
     table_copy = pltpu.make_async_copy(table_ref.at[:, own_half], table, table_sem)
-    for copy in stage_copies:
-        copy.wait()
+    pltpu.make_async_copy(stage, stage, stage_sem).wait()
     pl.semaphore_wait(barrier, awaited)
 
     def source(at, core):
-        k, start, count = plan[at]
+        k, start, count, _ = plan[at]
         return grad_ref.at[0, pl.ds(firsts[k], TOK_EDGE), pl.ds(core * half + start, count)]
 
     def place(at):
-        k, start, count = plan[at]
+        k, start, count, _ = plan[at]
         return halo.at[k, p, :, pl.ds(start, count)]
 
     def send_chunk(at):
+        k, _, _, group = plan[at]
         for core in range(n_dp):
             copy = remote(
                 stage.at[core] if at == 0 else source(at, core), place(at),
-                halo_send, halo_recv.at[at], (targets[plan[at][0]], core),
+                halo_send, halo_recv.at[group], (targets[k], core),
             )
-            if (at, core) in RELAYED:
-                pl.when(zone < RELAY_FROM[RELAYED.index((at, core))])(copy.start)
+            around = [
+                at_place(*key) for key, flows in RELAYED.items()
+                if (at, core) in [flow[1:3] for flow in flows]
+            ]
+            if at == FAR_NARROW:
+                around = [by_way(*key) for key, count in FAR_RELAYED.items() if core < count]
+            if around:
+                pl.when(jnp.logical_not(functools.reduce(jnp.logical_or, around)))(copy.start)
             else:
                 copy.start()
 
-    def relay_units(count):
-        return remote(
-            relayed.at[pl.ds(0, count)], relayed.at[pl.ds(0, count)],
-            relay_send, relay_recv, (opposite, p),
-        )
+    def relay_slots(first, count, send, recv):
+        slots = relayed.at[pl.ds(first, count)]
+        return remote(slots, slots, send, recv, (partner, p))
+
+    def by_way(quarter, core):
+        here = jnp.logical_and(far_quarter == quarter, set_bits[1] == 1)
+        return jnp.logical_and(here, p == core)
 
     def send_ids(k):
         for core in range(n_dp):
@@ -155,11 +191,14 @@
                 halo_id_send, halo_id_recv, (targets[k], core),
             ).start()
 
-    for unit, (at, core) in enumerate(RELAYED):
-        copy = remote(
-            source(at, core), relayed.at[unit], halo_send, relay_recv, (beyond, p)
-        )
-        pl.when(zone >= RELAY_FROM[unit])(copy.start)
+    for key, flows in RELAYED.items():
+        @pl.when(at_place(*key))
+        def _():
+            for slot, at, core in flows:
+                remote(
+                    source(at, core), relayed.at[slot], halo_send, relay_recv, (relay, p)
+                ).start()
+
     send_chunk(0)
     send_chunk(1)
     mate_copy = remote(
@@ -181,29 +220,41 @@
         )
 
     for k in range(1, bits):
-        if k == 1:
-            tell(k)
-        else:
-            pl.when(set_bits[k] == 1)(functools.partial(tell, k))
+        pl.when(set_bits[k] == 1)(functools.partial(tell, k))
         pl.semaphore_wait(known_sem.at[k - 1], 1)
-        if k > 1:
-            pl.when(set_bits[k] == 0)(functools.partial(tell, k))
+        pl.when(set_bits[k] == 0)(functools.partial(tell, k))
     send_ids(1)
 
-    for owner in range(2):
-        units = [unit for unit in range(len(RELAYED)) if RELAY_FROM[unit] <= 3 - owner]
-
-        @pl.when(zone == owner)
+    for key, count in FAR_RELAYED.items():
+        @pl.when(by_way(*key))
         def _():
-            relay_units(len(units)).wait_recv()
-            for unit in units:
-                at, core = RELAYED[unit]
+            for core in range(count):
                 remote(
-                    relayed.at[unit], place(at), relay_send, halo_recv.at[at], (opposite, core)
+                    source(FAR_NARROW, core), relayed.at[SLOTS + core], halo_send, far_recv, (via, p)
                 ).start()
 
-    for at in range(2, len(plan)):
+    for at in (2, FAR_NARROW, 3, 4, 5):
         send_chunk(at)
+    for (quarter, second, core), flows in RELAYED.items():
+        @pl.when(at_place(3 - quarter, second, core))
+        def _():
+            relay_slots(0, len(flows), relay_send, relay_recv).wait_recv()
+            for slot, at, target in flows:
+                remote(
+                    relayed.at[slot], place(at), relay_send, halo_recv.at[plan[at][3]],
+                    (beyond, target),
+                ).start()
+
+    def forward_far():
+        for (quarter, core), count in FAR_RELAYED.items():
+            @pl.when(at_place(quarter, 0, core))
+            def _():
+                relay_slots(SLOTS, count, far_send, far_recv).wait_recv()
+                for target in range(count):
+                    remote(
+                        relayed.at[SLOTS + target], place(FAR_NARROW), far_send,
+                        halo_recv.at[plan[FAR_NARROW][3]], (partner, target),
+                    ).start()
 
     own_start = v * rows
 
@@ -230,6 +281,10 @@
 
     window_ids = local(jnp.concatenate([own_ids[...], mate_ids[...]], axis=1))
     for block in range(blocks):
+        if block == 1:
+            forward_far()
+            for at in (6, 7):
+                send_chunk(at)
         picked = onehot(window_ids, block * EDGE, EDGE)
 
         @pl.loop(0, half // COLS)
@@ -246,17 +301,19 @@
         ids = local(jnp.concatenate([halo_ids[k, core] for core in range(n_dp)], axis=1))
         picks.append(onehot(ids, bases[k], EDGE))
     table_copy.wait()
-    for at, (k, start, count) in enumerate(plan):
-        here = pl.ds(start, count)
-        arrived = halo.at[k, :, :, here]
-        remote(arrived, arrived, halo_send, halo_recv.at[at], (partner, p)).wait_recv()
-        part = jnp.dot(
-            picks[k], halo[k, :, :, here].reshape(n_dp * TOK_EDGE, count),
-            preferred_element_type=jnp.float32,
-        )
-        total = grad[pl.ds(bases[k], EDGE), here] + part
-        grad[pl.ds(bases[k], EDGE), here] = total
-        add_squares(total)
+    for group, (k, first, size) in enumerate(groups_of(plan)):
+        arrived = halo.at[k, :, :, pl.ds(first, size)]
+        remote(arrived, arrived, halo_send, halo_recv.at[group], (partner, p)).wait_recv()
+        for start in range(first, first + size, PIECE):
+            count = min(PIECE, first + size - start)
+            here = pl.ds(start, count)
+            part = jnp.dot(
+                picks[k], halo[k, :, :, here].reshape(n_dp * TOK_EDGE, count),
+                preferred_element_type=jnp.float32,
+            )
+            total = grad[pl.ds(bases[k], EDGE), here] + part
+            grad[pl.ds(bases[k], EDGE), here] = total
+            add_squares(total)
 
     sums[me] = jnp.sum(square[...], axis=0, keepdims=True)
     for w in range(n_vocab):
@@ -265,9 +322,14 @@
             pl.when(me != w * n_dp + core)(copy.start)
     remote(halo, halo, halo_send, halo_recv.at[0], (partner, p)).wait_send()
     remote(halo_ids, halo_ids, halo_id_send, halo_id_recv, (partner, p)).wait_send()
-    for owner in range(2):
-        count = sum(start <= 3 - owner for start in RELAY_FROM)
-        pl.when(zone == owner)(relay_units(count).wait_send)
+    for (quarter, second, core), flows in RELAYED.items():
+        pl.when(at_place(3 - quarter, second, core))(
+            relay_slots(0, len(flows), relay_send, relay_recv).wait_send
+        )
+    for (quarter, core), count in FAR_RELAYED.items():
+        pl.when(at_place(quarter, 0, core))(
+            relay_slots(SLOTS, count, far_send, far_recv).wait_send
+        )
     others = sums.at[pl.ds(0, n - 1)]
     all_sums = remote(others, others, sum_send, sum_recv, (partner, p))
     all_sums.wait_recv()
@@ -322,7 +384,7 @@
                 pltpu.VMEM((n_dp * tokens, half), jnp.bfloat16),
                 pltpu.VMEM((2, n_dp, TOK_EDGE, half), jnp.bfloat16),
                 pltpu.VMEM((n_dp, TOK_EDGE, plan[0][2]), jnp.bfloat16),
-                pltpu.VMEM((len(RELAYED), TOK_EDGE, plan[RELAYED[0][0]][2]), jnp.bfloat16),
+                pltpu.VMEM((SLOTS + max(FAR_RELAYED.values()), TOK_EDGE, 128), jnp.bfloat16),
                 pltpu.VMEM((1, tokens), jnp.int32),
                 pltpu.VMEM((1, tokens), jnp.int32),
                 pltpu.VMEM((2, n_dp, 1, TOK_EDGE), jnp.int32),
@@ -331,11 +393,13 @@
                 pltpu.SemaphoreType.DMA,
                 pltpu.SemaphoreType.DMA,
                 pltpu.SemaphoreType.DMA,
-                pltpu.SemaphoreType.DMA((n_dp,)),
+                pltpu.SemaphoreType.DMA,
                 pltpu.SemaphoreType.DMA((2,)),
                 pltpu.SemaphoreType.DMA((2,)),
                 pltpu.SemaphoreType.DMA,
-                pltpu.SemaphoreType.DMA((len(plan),)),
+                pltpu.SemaphoreType.DMA((len(groups_of(plan)),)),
+                pltpu.SemaphoreType.DMA,
+                pltpu.SemaphoreType.DMA,
                 pltpu.SemaphoreType.DMA,
                 pltpu.SemaphoreType.DMA,
                 pltpu.SemaphoreType.DMA,

time: 58.3 us -> 57.7 us (0.990)
  Pallas kernels: 57.5 us -> 56.9 us
where the time goes in v3:
time: 57.7 us; the launch traced here: 57.6 us
  Pallas kernels  56.9 us (99%)
  between operations  0.64 us (1%)
    pallas_call x1, Pallas kernels, body(): pl.pallas_call(functools.partial(kernel, (n_vocab, n_dp)), name='clipped_...  54.9 us
    pallas_call x1, Pallas kernels, body(): pl.pallas_call(update, name='clipped_step', out_shape=(jax.ShapeDtypeStru...  2.03 us

profile of v3, /device:TPU:0, one launch (start us, length us, event | category | flops | bytes accessed | tf_op | source)
XLA Modules:
  0.0 57.6 jit_solution(4146801485883640209)
XLA Ops:
  0.6 54.9 %clipped_update.1 = (f32[1024,2048]{1,0:T(8,128)S(1)}, bf16[1024,2048]{1,0:T(8,128)(2,1)S(1)}, f32[8,128]{1,0:T(8,128)S(1)}) custom-call(bf16[1024,4096]{1,0:T(8,128)(2,1)} %table_ref.1, s32[1,1024]{1,0:T(1,128)} %ids_ref.1, bf16[1,1024,4096]{2,1,0:T(8,128)(2,1)} %grad_ref.1), custom_call_target="tpu_custom_call" | custom-call | tf_op jit(solution)/shard_map/clipped_update/pallas_call | solution.py:373
  55.5 2.0 %clipped_step.1 = (bf16[1024,2048]{1,0:T(8,128)(2,1)}, f32[1]{0:T(128)}) custom-call(f32[1024,2048]{1,0:T(8,128)S(1)} %get-tuple-element.5.grad, bf16[1024,2048]{1,0:T(8,128)(2,1)S(1)} %get-tuple-element.6.table, f32[8,128]{1,0:T(8,128)S(1)} %get-tuple-element.7.norm_ref), custom_call_target="tpu_custom_call" | custom-call | tf_op jit(solution)/shard_map/clipped_step/pallas_call | solution.py:415

commit v4 on v3

--- a/solution.py
+++ b/solution.py
@@ -42,8 +42,8 @@
         (1, 0, half - narrow, 1),
         (0, quarter + 2 * narrow, narrow, 2),
         (0, quarter + 3 * narrow, narrow, 3),
-        (0, 2 * quarter, quarter, 4),
-        (0, 3 * quarter, quarter - narrow, 5),
+        (0, 2 * quarter, 2 * quarter - 2 * narrow, 4),
+        (0, half - 2 * narrow, narrow, 5),
         (0, half - narrow, narrow, 7),
         (1, half - narrow, narrow, 6),
     )
@@ -158,9 +158,9 @@
         k, start, count, _ = plan[at]
         return halo.at[k, p, :, pl.ds(start, count)]
 
-    def send_chunk(at):
+    def send_chunk(at, cores=tuple(range(n_dp))):
         k, _, _, group = plan[at]
-        for core in range(n_dp):
+        for core in cores:
             copy = remote(
                 stage.at[core] if at == 0 else source(at, core), place(at),
                 halo_send, halo_recv.at[group], (targets[k], core),
@@ -283,8 +283,9 @@
     for block in range(blocks):
         if block == 1:
             forward_far()
-            for at in (6, 7):
-                send_chunk(at)
+            for core in range(n_dp):
+                for at in (6, 7):
+                    send_chunk(at, (core,))
         picked = onehot(window_ids, block * EDGE, EDGE)
 
         @pl.loop(0, half // COLS)

time: 57.7 us -> 57.5 us (level)
  no operation moved by 1% of the time
where the time goes in v4:
time: 57.5 us; the launch traced here: 57.3 us
  Pallas kernels  56.7 us (99%)
  between operations  0.64 us (1%)
    pallas_call x1, Pallas kernels, body(): pl.pallas_call(functools.partial(kernel, (n_vocab, n_dp)), name='clipped_...  54.7 us
    pallas_call x1, Pallas kernels, body(): pl.pallas_call(update, name='clipped_step', out_shape=(jax.ShapeDtypeStru...  2.03 us

profile of v4, /device:TPU:0, one launch (start us, length us, event | category | flops | bytes accessed | tf_op | source)
XLA Modules:
  0.0 57.3 jit_solution(13377776018129956637)
XLA Ops:
  0.6 54.7 %clipped_update.1 = (f32[1024,2048]{1,0:T(8,128)S(1)}, bf16[1024,2048]{1,0:T(8,128)(2,1)S(1)}, f32[8,128]{1,0:T(8,128)S(1)}) custom-call(bf16[1024,4096]{1,0:T(8,128)(2,1)} %table_ref.1, s32[1,1024]{1,0:T(1,128)} %ids_ref.1, bf16[1,1024,4096]{2,1,0:T(8,128)(2,1)} %grad_ref.1), custom_call_target="tpu_custom_call" | custom-call | tf_op jit(solution)/shard_map/clipped_update/pallas_call | solution.py:374
  55.3 2.0 %clipped_step.1 = (bf16[1024,2048]{1,0:T(8,128)(2,1)}, f32[1]{0:T(128)}) custom-call(f32[1024,2048]{1,0:T(8,128)S(1)} %get-tuple-element.5.grad, bf16[1024,2048]{1,0:T(8,128)(2,1)S(1)} %get-tuple-element.6.table, f32[8,128]{1,0:T(8,128)S(1)} %get-tuple-element.7.norm_ref), custom_call_target="tpu_custom_call" | custom-call | tf_op jit(solution)/shard_map/clipped_step/pallas_call | solution.py:416

commit v5 on v4

--- a/solution.py
+++ b/solution.py
@@ -30,7 +30,7 @@
 }
 SLOTS = 2
 FAR_NARROW = 8
-FAR_RELAYED = {(0, 0): 1, (0, 1): 1, (1, 0): 1, (1, 1): 1, (2, 0): 1, (3, 0): 1}
+FAR_RELAYED = {(0, 0): 1, (1, 0): 1, (1, 1): 1, (2, 0): 1, (3, 0): 1}
 
 
 def chunk_plan(half):
@@ -337,8 +337,7 @@
 
     total = jnp.sum(jnp.sum(sums[...], axis=0), axis=1, keepdims=True)
     rms = jnp.sqrt(total / (n_vocab * rows * width))
-    clip_scale = 1.0 / jnp.maximum(1.0, rms / norm_limit)
-    norm_ref[0:1, :] = jnp.broadcast_to(step_rate * clip_scale, (1, 128))
+    norm_ref[0:1, :] = jnp.broadcast_to(step_rate / jnp.maximum(1.0, rms / norm_limit), (1, 128))
     norm_ref[1:2, :] = jnp.broadcast_to(rms, (1, 128))
     all_sums.wait_send()
 
@@ -347,7 +346,7 @@
     rms_held[0] = norm_ref[1, 0]
     rms_copy = pltpu.make_async_copy(rms_held, rms_ref, rms_sem)
     rms_copy.start()
-    rate = norm_ref[0:1, 0:1]
+    rate = jnp.concatenate([norm_ref[0:1, :]] * (STORE_COLS // 128), axis=1)
     for block in range(grad.shape[0] // STORE_ROWS):
         here = pl.ds(block * STORE_ROWS, STORE_ROWS)
         for start in range(0, grad.shape[1], STORE_COLS):

time: 57.5 us -> 57.4 us (level)
  no operation moved by 1% of the time
where the time goes in v5:
time: 57.4 us; the launch traced here: 57.2 us
  Pallas kernels  56.6 us (99%)
  between operations  0.64 us (1%)
    pallas_call x1, Pallas kernels, body(): pl.pallas_call(functools.partial(kernel, (n_vocab, n_dp)), name='clipped_...  54.6 us
    pallas_call x1, Pallas kernels, body(): pl.pallas_call(update, name='clipped_step', out_shape=(jax.ShapeDtypeStru...  2 us

profile of v5, /device:TPU:0, one launch (start us, length us, event | category | flops | bytes accessed | tf_op | source)
XLA Modules:
  0.0 57.2 jit_solution(15844994571901900939)
XLA Ops:
  0.6 54.6 %clipped_update.1 = (f32[1024,2048]{1,0:T(8,128)S(1)}, bf16[1024,2048]{1,0:T(8,128)(2,1)S(1)}, f32[8,128]{1,0:T(8,128)S(1)}) custom-call(bf16[1024,4096]{1,0:T(8,128)(2,1)} %table_ref.1, s32[1,1024]{1,0:T(1,128)} %ids_ref.1, bf16[1,1024,4096]{2,1,0:T(8,128)(2,1)} %grad_ref.1), custom_call_target="tpu_custom_call" | custom-call | tf_op jit(solution)/shard_map/clipped_update/pallas_call | solution.py:373
  55.2 2.0 %clipped_step.1 = (bf16[1024,2048]{1,0:T(8,128)(2,1)}, f32[1]{0:T(128)}) custom-call(f32[1024,2048]{1,0:T(8,128)S(1)} %get-tuple-element.5.grad, bf16[1024,2048]{1,0:T(8,128)(2,1)S(1)} %get-tuple-element.6.table, f32[8,128]{1,0:T(8,128)S(1)} %get-tuple-element.7.norm_ref), custom_call_target="tpu_custom_call" | custom-call | tf_op jit(solution)/shard_map/clipped_step/pallas_call | solution.py:415

commit v6 on v5

--- a/solution.py
+++ b/solution.py
@@ -59,7 +59,7 @@
 
 def kernel(sizes, table_ref, ids_ref, grad_ref, grad, table, norm_ref,
            toks, halo, stage, relayed, own_ids, mate_ids, halo_ids, square, sums,
-           own_sem, own_id_sem, table_sem, stage_sem, mate_sem, mate_id_sem,
+           own_sem, own_id_sem, stage_sem, mate_sem, mate_id_sem,
            halo_send, halo_recv, halo_id_send, halo_id_recv, sum_send, sum_recv,
            relay_send, relay_recv, far_send, far_recv, known_sem):
     n_vocab, n_dp = sizes
@@ -146,7 +146,7 @@
     own_copy.start()
     own_id_copy = pltpu.make_async_copy(ids_ref, own_ids, own_id_sem)
     own_id_copy.start()
-    table_copy = pltpu.make_async_copy(table_ref.at[:, own_half], table, table_sem)
+    table_copy = pltpu.make_async_copy(table_ref.at[:, own_half], table, stage_sem)
     pltpu.make_async_copy(stage, stage, stage_sem).wait()
     pl.semaphore_wait(barrier, awaited)
 
@@ -343,9 +343,6 @@
 
 
 def update(grad, table, norm_ref, out_ref, rms_ref, outbuf, rms_held, out_sem, rms_sem):
-    rms_held[0] = norm_ref[1, 0]
-    rms_copy = pltpu.make_async_copy(rms_held, rms_ref, rms_sem)
-    rms_copy.start()
     rate = jnp.concatenate([norm_ref[0:1, :]] * (STORE_COLS // 128), axis=1)
     for block in range(grad.shape[0] // STORE_ROWS):
         here = pl.ds(block * STORE_ROWS, STORE_ROWS)
@@ -354,6 +351,9 @@
             moved = table[at].astype(jnp.float32) - rate * grad[at]
             outbuf[at] = moved.astype(jnp.bfloat16)
         pltpu.make_async_copy(outbuf.at[here, :], out_ref.at[here, :], out_sem).start()
+    rms_held[0] = norm_ref[1, 0]
+    rms_copy = pltpu.make_async_copy(rms_held, rms_ref, rms_sem)
+    rms_copy.start()
     pltpu.make_async_copy(outbuf, out_ref, out_sem).wait()
     rms_copy.wait()
 
@@ -393,7 +393,6 @@
                 pltpu.SemaphoreType.DMA,
                 pltpu.SemaphoreType.DMA,
                 pltpu.SemaphoreType.DMA,
-                pltpu.SemaphoreType.DMA,
                 pltpu.SemaphoreType.DMA((2,)),
                 pltpu.SemaphoreType.DMA((2,)),
                 pltpu.SemaphoreType.DMA,

time: 57.4 us -> 57.4 us (level)
  no operation moved by 1% of the time
where the time goes in v6:
time: 57.4 us; the launch traced here: 57.2 us
  Pallas kernels  56.6 us (99%)
  between operations  0.64 us (1%)
    pallas_call x1, Pallas kernels, body(): pl.pallas_call(functools.partial(kernel, (n_vocab, n_dp)), name='clipped_...  54.6 us
    pallas_call x1, Pallas kernels, body(): pl.pallas_call(update, name='clipped_step', out_shape=(jax.ShapeDtypeStru...  2 us

profile of v6, /device:TPU:0, one launch (start us, length us, event | category | flops | bytes accessed | tf_op | source)
XLA Modules:
  0.0 57.2 jit_solution(15488503954480943519)
XLA Ops:
  0.6 54.6 %clipped_update.1 = (f32[1024,2048]{1,0:T(8,128)S(1)}, bf16[1024,2048]{1,0:T(8,128)(2,1)S(1)}, f32[8,128]{1,0:T(8,128)S(1)}) custom-call(bf16[1024,4096]{1,0:T(8,128)(2,1)} %table_ref.1, s32[1,1024]{1,0:T(1,128)} %ids_ref.1, bf16[1,1024,4096]{2,1,0:T(8,128)(2,1)} %grad_ref.1), custom_call_target="tpu_custom_call" | custom-call | tf_op jit(solution)/shard_map/clipped_update/pallas_call | solution.py:373
  55.2 2.0 %clipped_step.1 = (bf16[1024,2048]{1,0:T(8,128)(2,1)}, f32[1]{0:T(128)}) custom-call(f32[1024,2048]{1,0:T(8,128)S(1)} %get-tuple-element.5.grad, bf16[1024,2048]{1,0:T(8,128)(2,1)S(1)} %get-tuple-element.6.table, f32[8,128]{1,0:T(8,128)S(1)} %get-tuple-element.7.norm_ref), custom_call_target="tpu_custom_call" | custom-call | tf_op jit(solution)/shard_map/clipped_step/pallas_call | solution.py:414
